TPU v7x, 256 devices: a whole 4x4x8 slice. The times are simulated.
256 devices in a mesh: row: 16 (over x_hi, z), col: 8 (over x_lo, y), rep: 2 (over core).
Axes of the slice: x: 4 (x_hi: 2, x_lo: 2; x = x_hi * 2 + x_lo), y: 4, z: 8, core: 2. Of those that a mesh axis runs over, the one named last changes fastest.
Arguments:
- matrix: float32 [16384, 16384], P('row', 'col'), may hold values from -0.125 to 0.125
- vectors: float32 [64, 16384], P('rep', 'row'), may hold values from -0.3 to 0.3
Outputs:
- result: float32 [64, 16384], P('rep', 'row')
All inputs are finite; a program needn't handle non-finite values.
Results may differ from a plain program's by a relative error of at most 0.00011.
Values sent between devices are 32-bit elements; how exact they have to be, the bound alone decides.
A program may use at most 64 MiB of HBM per device.

v0:
```python
import jax
import jax.numpy as jnp
from jax import lax
from jax.sharding import PartitionSpec as P

TERMS = 6
STEPS = 1


def from_root(shard, axis, root):
    return lax.dynamic_index_in_dim(lax.all_gather(shard, axis), root, 0, keepdims=False)


def copy_for_each(shard, axis):
    count = lax.axis_size(axis)
    return lax.all_to_all(
        jnp.broadcast_to(shard[None], (count, *shard.shape)), axis, 0, 0, tiled=True
    )


def over_copies(shard, axis):
    return copy_for_each(shard, axis).sum(axis=0)


def apply_matrix(current, matrix):
    fanout = lax.axis_size("row") // lax.axis_size("col")
    column_index = lax.axis_index("col")
    pieces = [from_root(current, "row", column_index * fanout + which) for which in range(fanout)]
    operand = jnp.concatenate(pieces, axis=1)
    partial_value = lax.dot_general(
        operand,
        matrix,
        (((1,), (1,)), ((), ())),
        precision=lax.Precision.HIGHEST,
        preferred_element_type=jnp.float32,
    )
    return over_copies(partial_value, "col")


def local(matrix, vectors):
    summand = vectors
    running = vectors
    for degree in range(1, TERMS + 1):
        summand = apply_matrix(summand, matrix) / float(degree * STEPS)
        running = running + summand
    return running


def solution(mesh):
    placed = (P("row", "col"), P("rep", "row"))
    return jax.shard_map(
        local, mesh=mesh, in_specs=placed, out_specs=P("rep", "row"), check_vma=False
    )
```

profile of v0, /device:TPU:1, one launch (start us, length us, event | category | flops | bytes accessed | tf_op | source)
XLA Modules:
  0.0 673.0 jit_solution(11237662189762884529)
XLA Ops:
  6.5 0.0 all-gather.13.cloned.1.call-start
  6.5 0.7 all-gather.13.cloned.1.call-update
  7.3 0.0 all-gather.15.cloned.1.call-start
  7.3 88.1 %all-gather.13.cloned.1.call-done = f32[512,1024]{1,0:T(8,128)} async-done(((f32[32,1024]{1,0:T(8,128)}), f32[512,1024]{1,0:T(8,128)}) %all-gather.13.cloned.1.call-update) | async-done | bytes 2097168 | tf_op jit(solution)/shard_map/all_gather | solution.py:11
  95.5 1.0 dynamic-slice_bitcast_fusion.11
  96.4 10.0 %fusion = f32[32,1024]{1,0:T(8,128)S(1)} fusion(f32[1024,2048]{1,0:T(8,128)} %param.2, f32[32,1024]{1,0:T(8,128)S(1)} %get-tuple-element.16, f32[32,1024]{1,0:T(8,128)S(1)} %get-tuple-element.15), kind=kOutput, calls=%fused_computation | convolution fusion | flops 805371904 | bytes 8781824 | tf_op jit(solution)/shard_map/dot_general | solution.py:30
  106.4 0.1 broadcast_in_dim.12
  106.5 14.1 %all_to_all.30 = f32[8,32,1024]{2,1,0:T(8,128)S(1)} all-to-all(f32[8,32,1024]{2,1,0:T(8,128)S(1)} %broadcast_in_dim.12), channel_id=1, replica_groups=mesh['row'=16,'col'=8,'rep'=2] {'col'}, dimensions={0} | all-to-all | bytes 2097152 | tf_op jit(solution)/shard_map/all_to_all | solution.py:16
  120.7 0.7 reduce_sum.54
  121.4 0.0 all-gather.15.cloned.1.call-update
  121.4 0.0 all-gather.17.cloned.1.call-start
  121.5 82.9 %all-gather.15.cloned.1.call-done = f32[512,1024]{1,0:T(8,128)} async-done(((f32[32,1024]{1,0:T(8,128)}), f32[512,1024]{1,0:T(8,128)}) %all-gather.15.cloned.1.call-update) | async-done | bytes 2097168 | tf_op jit(solution)/shard_map/all_gather | solution.py:11
  204.3 1.0 dynamic-slice_bitcast_fusion.9
  205.3 10.0 %fusion.4 = f32[32,1024]{1,0:T(8,128)S(1)} fusion(f32[1024,2048]{1,0:T(8,128)} %param.2, f32[32,1024]{1,0:T(8,128)S(1)} %get-tuple-element.14, f32[32,1024]{1,0:T(8,128)S(1)} %get-tuple-element.13), kind=kOutput, calls=%fused_computation.4 | convolution fusion | flops 805371904 | bytes 8781824 | tf_op jit(solution)/shard_map/dot_general | solution.py:30
  215.3 0.1 broadcast_in_dim.13
  215.4 14.1 %all_to_all.31 = f32[8,32,1024]{2,1,0:T(8,128)S(1)} all-to-all(f32[8,32,1024]{2,1,0:T(8,128)S(1)} %broadcast_in_dim.13), channel_id=1, replica_groups=mesh['row'=16,'col'=8,'rep'=2] {'col'}, dimensions={0} | all-to-all | bytes 2097152 | tf_op jit(solution)/shard_map/all_to_all | solution.py:16
  229.6 0.1 reduce_sum.55
  229.6 0.7 broadcast_multiply_fusion.3
  230.3 0.0 all-gather.17.cloned.1.call-update
  230.3 0.0 all-gather.19.cloned.1.call-start
  230.4 82.9 %all-gather.17.cloned.1.call-done = f32[512,1024]{1,0:T(8,128)} async-done(((f32[32,1024]{1,0:T(8,128)}), f32[512,1024]{1,0:T(8,128)}) %all-gather.17.cloned.1.call-update) | async-done | bytes 2097168 | tf_op jit(solution)/shard_map/all_gather | solution.py:11
  313.2 1.0 dynamic-slice_bitcast_fusion.7
  314.2 10.0 %fusion.8 = f32[32,1024]{1,0:T(8,128)S(1)} fusion(f32[1024,2048]{1,0:T(8,128)} %param.2, f32[32,1024]{1,0:T(8,128)S(1)} %get-tuple-element.12, f32[32,1024]{1,0:T(8,128)S(1)} %get-tuple-element.11), kind=kOutput, calls=%fused_computation.8 | convolution fusion | flops 805371904 | bytes 8781824 | tf_op jit(solution)/shard_map/dot_general | solution.py:30
  324.2 0.1 broadcast_in_dim.14
  324.3 14.1 %all_to_all.32 = f32[8,32,1024]{2,1,0:T(8,128)S(1)} all-to-all(f32[8,32,1024]{2,1,0:T(8,128)S(1)} %broadcast_in_dim.14), channel_id=1, replica_groups=mesh['row'=16,'col'=8,'rep'=2] {'col'}, dimensions={0} | all-to-all | bytes 2097152 | tf_op jit(solution)/shard_map/all_to_all | solution.py:16
  338.5 0.1 reduce_sum.56
  338.5 0.7 broadcast_multiply_fusion.2
  339.2 0.0 all-gather.19.cloned.1.call-update
  339.2 0.2 all-gather.21.cloned.1.call-start
  339.5 82.7 %all-gather.19.cloned.1.call-done = f32[512,1024]{1,0:T(8,128)} async-done(((f32[32,1024]{1,0:T(8,128)}), f32[512,1024]{1,0:T(8,128)}) %all-gather.19.cloned.1.call-update) | async-done | bytes 2097168 | tf_op jit(solution)/shard_map/all_gather | solution.py:11
  422.1 1.0 dynamic-slice_bitcast_fusion.5
  423.1 10.0 %fusion.12 = f32[32,1024]{1,0:T(8,128)S(1)} fusion(f32[1024,2048]{1,0:T(8,128)} %param.2, f32[32,1024]{1,0:T(8,128)S(1)} %get-tuple-element.10, f32[32,1024]{1,0:T(8,128)S(1)} %get-tuple-element.9), kind=kOutput, calls=%fused_computation.12 | convolution fusion | flops 805371904 | bytes 8781824 | tf_op jit(solution)/shard_map/dot_general | solution.py:30
  433.1 0.1 broadcast_in_dim.15
  433.2 14.1 %all_to_all.33 = f32[8,32,1024]{2,1,0:T(8,128)S(1)} all-to-all(f32[8,32,1024]{2,1,0:T(8,128)S(1)} %broadcast_in_dim.15), channel_id=1, replica_groups=mesh['row'=16,'col'=8,'rep'=2] {'col'}, dimensions={0} | all-to-all | bytes 2097152 | tf_op jit(solution)/shard_map/all_to_all | solution.py:16
  447.4 0.1 reduce_sum.57
  447.4 0.7 broadcast_multiply_fusion.1
  448.1 0.0 all-gather.21.cloned.1.call-update
  448.1 0.0 all-gather.23.cloned.1.call-start
  448.2 82.9 %all-gather.21.cloned.1.call-done = f32[512,1024]{1,0:T(8,128)} async-done(((f32[32,1024]{1,0:T(8,128)}), f32[512,1024]{1,0:T(8,128)}) %all-gather.21.cloned.1.call-update) | async-done | bytes 2097168 | tf_op jit(solution)/shard_map/all_gather | solution.py:11
  531.0 1.0 dynamic-slice_bitcast_fusion.3
  532.0 10.0 %fusion.16 = f32[32,1024]{1,0:T(8,128)S(1)} fusion(f32[1024,2048]{1,0:T(8,128)} %param.2, f32[32,1024]{1,0:T(8,128)S(1)} %get-tuple-element.8, f32[32,1024]{1,0:T(8,128)S(1)} %get-tuple-element.7), kind=kOutput, calls=%fused_computation.16 | convolution fusion | flops 805371904 | bytes 8781824 | tf_op jit(solution)/shard_map/dot_general | solution.py:30
  542.0 0.1 broadcast_in_dim.16
  542.1 0.0 copy-start
  542.1 0.0 copy-start.1
  542.2 14.3 %all_to_all.34 = f32[8,32,1024]{2,1,0:T(8,128)S(1)} all-to-all(f32[8,32,1024]{2,1,0:T(8,128)S(1)} %broadcast_in_dim.16), channel_id=1, replica_groups=mesh['row'=16,'col'=8,'rep'=2] {'col'}, dimensions={0} | all-to-all | bytes 2097152 | tf_op jit(solution)/shard_map/all_to_all | solution.py:16
  556.4 0.1 reduce_sum.58
  556.5 0.7 broadcast_multiply_fusion
  557.2 0.0 all-gather.23.cloned.1.call-update
  557.2 82.9 %all-gather.23.cloned.1.call-done = f32[512,1024]{1,0:T(8,128)} async-done(((f32[32,1024]{1,0:T(8,128)}), f32[512,1024]{1,0:T(8,128)}) %all-gather.23.cloned.1.call-update) | async-done | bytes 2097168 | tf_op jit(solution)/shard_map/all_gather | solution.py:11
  640.1 1.0 dynamic-slice_bitcast_fusion.1
  641.1 10.0 %fusion.20 = f32[32,1024]{1,0:T(8,128)S(1)} fusion(f32[1024,2048]{1,0:T(8,128)} %param.2, f32[32,1024]{1,0:T(8,128)S(1)} %get-tuple-element.6, f32[32,1024]{1,0:T(8,128)S(1)} %get-tuple-element.5), kind=kOutput, calls=%fused_computation.20 | convolution fusion | flops 805371904 | bytes 8781824 | tf_op jit(solution)/shard_map/dot_general | solution.py:30
  651.1 0.1 broadcast_in_dim.17
  651.2 14.1 %all_to_all.35 = f32[8,32,1024]{2,1,0:T(8,128)S(1)} all-to-all(f32[8,32,1024]{2,1,0:T(8,128)S(1)} %broadcast_in_dim.17), channel_id=1, replica_groups=mesh['row'=16,'col'=8,'rep'=2] {'col'}, dimensions={0} | all-to-all | bytes 2097152 | tf_op jit(solution)/shard_map/all_to_all | solution.py:16
  665.3 0.1 reduce_sum.59
  665.4 0.0 copy-done
  665.4 0.0 copy-done.1
  665.4 0.7 multiply_add_fusion
Async XLA Ops:
  6.5 88.9 %all-gather.13.cloned.1.call-start = ((), (), s32[]{:S(2)}) async-start(), calls=%async_computation.6 | async-start | bytes 2228224 | tf_op jit(solution)/shard_map/all_gather | solution.py:11
  7.3 197.1 %all-gather.15.cloned.1.call-start = ((), (), s32[]{:S(2)}) async-start(), calls=%async_computation.7 | async-start | bytes 2228224 | tf_op jit(solution)/shard_map/all_gather | solution.py:11
  121.4 191.8 %all-gather.17.cloned.1.call-start = ((), (), s32[]{:S(2)}) async-start(), calls=%async_computation.8 | async-start | bytes 2228224 | tf_op jit(solution)/shard_map/all_gather | solution.py:11
  230.3 191.8 %all-gather.19.cloned.1.call-start = ((), (), s32[]{:S(2)}) async-start(), calls=%async_computation.9 | async-start | bytes 2228224 | tf_op jit(solution)/shard_map/all_gather | solution.py:11
  339.2 191.8 %all-gather.21.cloned.1.call-start = ((), (), s32[]{:S(2)}) async-start(), calls=%async_computation.10 | async-start | bytes 2228224 | tf_op jit(solution)/shard_map/all_gather | solution.py:11
  448.1 192.0 %all-gather.23.cloned.1.call-start = ((), (), s32[]{:S(2)}) async-start(), calls=%async_computation.11 | async-start | bytes 2228224 | tf_op jit(solution)/shard_map/all_gather | solution.py:11
  542.1 123.3 %copy-start = (f32[32,1024]{1,0:T(8,128)S(1)}, f32[32,1024]{1,0:T(8,128)}, u32[]{:S(2)}) copy-start(f32[32,1024]{1,0:T(8,128)} %reduce_sum.54) | copy-start | bytes 393220
  542.1 123.3 %copy-start.1 = (f32[32,1024]{1,0:T(8,128)S(1)}, f32[32,1024]{1,0:T(8,128)}, u32[]{:S(2)}) copy-start(f32[32,1024]{1,0:T(8,128)} %param.3) | copy-start | bytes 393220
Sparse Core Ops, SparseCore 0:
  9.9 85.4 all-gather.12
  121.5 82.7 all-gather.14
  230.4 82.7 all-gather.16
  339.4 82.7 all-gather.18
  448.3 82.7 all-gather.20
  557.3 82.7 all-gather.22
where the time goes:
time: 677 us; the launch traced here: 673 us
  waiting for transfers between devices  503 us (74%)
  blocking collectives  85 us (13%)
  matrix products  59.8 us (9%)
  between operations  13.6 us (2%)
    all_gather x6, waiting for transfers between devices, from_root(): lax.all_gather(shard, axis)  502 us
    all_to_all x6, blocking collectives, copy_for_each(): lax.all_to_all(jnp.broadcast_to(shard[None], (count, *shard.shape)), axis...  85 us
    dot_general x6, matrix products, apply_matrix(): lax.dot_general(operand, matrix, (((1,), (1,)), ((), ())), precision=lax....  59.8 us
  transfers between devices with their start and end apart: 6, of which 6 were waited for; matrix products, arithmetic and copies ran while one was open for 0% of the time, Pallas kernels for 0%

commit v1 on v0

v1 whole, which is shorter than its diff:
```python
import functools

import jax
import jax.numpy as jnp
from jax import lax
from jax.experimental import pallas as pl
from jax.experimental.pallas import tpu as pltpu
from jax.sharding import PartitionSpec as P

TERMS = 6
STEPS = 1
CHUNKS = 2
ROWS = 32 // CHUNKS
PIECE = 256
PIECES = 8
MESH = pl.DeviceIdType.MESH


def kernel(
    matrix_hbm,
    vectors_hbm,
    result_ref,
    stage,
    w_high,
    w_low,
    vectors_ref,
    start_piece,
    operand,
    partial_out,
    partial_in,
    summand,
    total,
    total_in,
    stage_sem,
    vectors_sem,
    piece_sem,
    operand_sem,
    partial_sem,
    total_sem,
    operand_send,
    partial_send,
    total_send,
):
    row, col, rep = lax.axis_index("row"), lax.axis_index("col"), lax.axis_index("rep")
    z, y = row % 8, col % 4
    x = (row // 8) * 2 + col // 4
    outer = (x == 0) | (x == 3)
    swapped = jnp.where(outer, x, 3 - x)
    parity = z % 2

    def device(dx, dy, dz):
        return ((dx // 2) * 8 + dz, (dx % 2) * 4 + dy, rep)

    def remote(dx, dy, dz):
        return (dx != x) | (dy != y) | (dz != z)

    partial_to = [
        (x // 2 + 2 * half, (y + step) % 4, z) for step in (2, 1, 3, 0) for half in (0, 1)
    ]
    partial_from = [(2 * (x % 2) + low, other, z) for other in range(4) for low in (0, 1)]
    operand_to = [(z // 2, (z + step) % 8) for step in (4, 3, 5, 2, 6, 1, 7, 0)]
    operand_from = [(other, 2 * y + which) for other in range(4) for which in (0, 1)]
    total_to = [(swapped, (y + step) % 4, z) for step in (2, 1, 3, 0)]

    def stage_copy(piece):
        return pltpu.make_async_copy(
            matrix_hbm.at[:, pl.ds(piece * PIECE, PIECE)], stage.at[piece], stage_sem.at[piece]
        )

    def piece_copy(chunk):
        return pltpu.make_async_copy(
            vectors_hbm.at[pl.ds(chunk * ROWS, ROWS), pl.ds(pl.multiple_of(y * PIECE, PIECE), PIECE)],
            start_piece.at[chunk],
            piece_sem.at[chunk],
        )

    vectors_copy = pltpu.make_async_copy(vectors_hbm, vectors_ref, vectors_sem)
    for chunk in range(CHUNKS):
        piece_copy(chunk).start()
    for piece in range(PIECES):
        stage_copy(piece).start()
    vectors_copy.start()

    barrier = pltpu.get_barrier_semaphore()
    greeted = partial_to + partial_from + total_to
    greeted += [(x, *rest) for rest in operand_to + operand_from]
    greeted += [(swapped, *rest) for rest in operand_to + operand_from]
    count = 0
    for place in greeted:
        there = remote(*place)

        @pl.when(there)
        def _():
            pl.semaphore_signal(barrier, inc=1, device_id=device(*place), device_id_type=MESH)

        count = count + there.astype(jnp.int32)
    pl.semaphore_wait(barrier, count)

    def send(source, target, send_sem, recv_sem, place):
        @pl.when(remote(*place))
        def _():
            pltpu.make_async_remote_copy(
                src_ref=source,
                dst_ref=target,
                send_sem=send_sem,
                recv_sem=recv_sem,
                device_id=device(*place),
                device_id_type=MESH,
            ).start()

    def send_operand(source, across, degree, chunk):
        slot = parity * 4 + y
        for rest in operand_to:
            send(
                source,
                operand.at[degree, chunk, slot],
                operand_send.at[degree, chunk],
                operand_sem.at[degree, chunk, slot],
                (across, *rest),
            )

    for chunk in range(CHUNKS):
        piece_copy(chunk).wait()
        send_operand(start_piece.at[chunk], swapped, 0, chunk)

        @pl.when(outer & (z // 2 == y))
        def _():
            operand[0, chunk, parity * 4 + y] = start_piece[chunk]

    for piece in range(PIECES):
        stage_copy(piece).wait()

        def split(block, _):
            at = pl.ds(pl.multiple_of(block * PIECE, PIECE), PIECE)
            turned = stage[piece, at, :].T
            high = turned.astype(jnp.bfloat16)
            w_high[piece, :, at] = high
            w_low[piece, :, at] = (turned - high.astype(jnp.float32)).astype(jnp.bfloat16)
            return 0

        lax.fori_loop(0, 1024 // PIECE, split, 0)

    total[...] = jnp.zeros_like(total)

    def multiply(degree, chunk):
        acc = jnp.zeros((ROWS, 1024), jnp.float32)
        for step in (0, 1, 3, 2):
            for which in (0, 1):
                other = (y + step) % 4
                slot = which * 4 + other
                arrival = pltpu.make_async_copy(
                    operand.at[degree - 1, chunk, slot],
                    operand.at[degree - 1, chunk, slot],
                    operand_sem.at[degree - 1, chunk, slot],
                )
                if step == 0:
                    own = (2 * y + which == z) & (outer | (degree > 1))
                    pl.when(jnp.logical_not(own))(arrival.wait)
                else:
                    arrival.wait()
                value = operand[degree - 1, chunk, slot]
                high = value.astype(jnp.bfloat16)
                low = (value - high.astype(jnp.float32)).astype(jnp.bfloat16)
                both = jnp.dot(
                    jnp.concatenate([high, low], axis=0),
                    w_high[slot],
                    preferred_element_type=jnp.float32,
                )
                small = jnp.dot(high, w_low[slot], preferred_element_type=jnp.float32)
                acc = acc + (both[:ROWS] + (both[ROWS:] + small))
        for piece in range(4):
            partial_out[degree - 1, chunk, piece] = acc[:, piece * PIECE : (piece + 1) * PIECE]
        slot = (x % 2) * 4 + y

        @pl.when(outer)
        def _():
            partial_in[degree - 1, chunk, slot] = partial_out[degree - 1, chunk, y]

        for place in partial_to:
            send(
                partial_out.at[degree - 1, chunk, place[1]],
                partial_in.at[degree - 1, chunk, slot],
                partial_send.at[degree - 1, chunk],
                partial_sem.at[degree - 1, chunk, slot],
                place,
            )

    def add_up(degree, chunk, scale):
        for low in (0, 1):
            for other in range(4):
                slot = low * 4 + other
                own = outer & (other == y) & (x % 2 == low)
                arrival = pltpu.make_async_copy(
                    partial_in.at[degree - 1, chunk, slot],
                    partial_in.at[degree - 1, chunk, slot],
                    partial_sem.at[degree - 1, chunk, slot],
                )
                pl.when(jnp.logical_not(own))(arrival.wait)
        value = partial_in[degree - 1, chunk, 0]
        for slot in range(1, PIECES):
            value = value + partial_in[degree - 1, chunk, slot]
        return value * scale

    def section(degree, _):
        scale = jnp.float32(1.0 / STEPS)
        for which in range(2, TERMS):
            scale = jnp.where(degree == which, jnp.float32(1.0 / (which * STEPS)), scale)
        for chunk in range(CHUNKS):
            multiply(degree, chunk)
        for chunk in range(CHUNKS):
            value = add_up(degree, chunk, scale)
            summand[degree, chunk] = value
            send_operand(summand.at[degree, chunk], x, degree, chunk)

            @pl.when(z // 2 == y)
            def _():
                operand[degree, chunk, parity * 4 + y] = value

            total[chunk] += value
        return 0

    lax.fori_loop(1, TERMS, section, 0)
    for chunk in range(CHUNKS):
        multiply(TERMS, chunk)
    vectors_copy.wait()
    for chunk in range(CHUNKS):
        total[chunk] += add_up(TERMS, chunk, jnp.float32(1.0 / (TERMS * STEPS)))

        @pl.when(outer)
        def _():
            total_in[chunk, y] = total[chunk]

        for place in total_to:
            send(
                total.at[chunk],
                total_in.at[chunk, y],
                total_send.at[chunk],
                total_sem.at[chunk, y],
                place,
            )
    for chunk in range(CHUNKS):
        at = pl.ds(chunk * ROWS, ROWS)
        for other in range(4):
            arrival = pltpu.make_async_copy(
                total_in.at[chunk, other], total_in.at[chunk, other], total_sem.at[chunk, other]
            )
            pl.when(jnp.logical_not(outer & (other == y)))(arrival.wait)
            columns = pl.ds(other * PIECE, PIECE)
            result_ref[at, columns] = vectors_ref[at, columns] + total_in[chunk, other]

    def sent(sem, buffer, all_but_one):
        def wait(number):
            part = buffer.at[pl.ds(0, number)]
            pltpu.make_async_copy(part, part, sem).wait()

        full = buffer.shape[0]
        pl.when(all_but_one)(lambda: wait(full - 1))
        pl.when(jnp.logical_not(all_but_one))(lambda: wait(full))

    at_home = z // 2 == y

    def finish(degree, _):
        for chunk in range(CHUNKS):
            sent(operand_send.at[degree, chunk], operand.at[degree, chunk], at_home & (outer | (degree > 0)))
            sent(partial_send.at[degree, chunk], partial_in.at[degree, chunk], outer)
        return 0

    lax.fori_loop(0, TERMS, finish, 0)
    for chunk in range(CHUNKS):
        sent(total_send.at[chunk], total_in.at[chunk], outer)


def local(matrix, vectors):
    dma = pltpu.SemaphoreType.DMA
    float32, bfloat16 = jnp.float32, jnp.bfloat16
    return pl.pallas_call(
        kernel,
        out_shape=jax.ShapeDtypeStruct(vectors.shape, float32),
        in_specs=[pl.BlockSpec(memory_space=pl.ANY)] * 2,
        out_specs=pl.BlockSpec(memory_space=pltpu.VMEM),
        scratch_shapes=[
            pltpu.VMEM((PIECES, 1024, PIECE), float32),
            pltpu.VMEM((PIECES, PIECE, 1024), bfloat16),
            pltpu.VMEM((PIECES, PIECE, 1024), bfloat16),
            pltpu.VMEM((32, 1024), float32),
            pltpu.VMEM((CHUNKS, ROWS, PIECE), float32),
            pltpu.VMEM((TERMS, CHUNKS, PIECES, ROWS, PIECE), float32),
            pltpu.VMEM((TERMS, CHUNKS, 4, ROWS, PIECE), float32),
            pltpu.VMEM((TERMS, CHUNKS, PIECES, ROWS, PIECE), float32),
            pltpu.VMEM((TERMS, CHUNKS, ROWS, PIECE), float32),
            pltpu.VMEM((CHUNKS, ROWS, PIECE), float32),
            pltpu.VMEM((CHUNKS, 4, ROWS, PIECE), float32),
            dma((PIECES,)),
            dma,
            dma((CHUNKS,)),
            dma((TERMS, CHUNKS, PIECES)),
            dma((TERMS, CHUNKS, PIECES)),
            dma((CHUNKS, 4)),
            dma((TERMS, CHUNKS)),
            dma((TERMS, CHUNKS)),
            dma((CHUNKS,)),
        ],
        compiler_params=pltpu.CompilerParams(
            collective_id=0, has_side_effects=True, vmem_limit_bytes=48 * 2**20
        ),
    )(matrix, vectors)


def solution(mesh):
    return jax.shard_map(
        local,
        mesh=mesh,
        in_specs=(P("row", "col"), P("rep", "row")),
        out_specs=P("rep", "row"),
        check_vma=False,
    )
```

time: 677 us -> 93.7 us (0.14)
  the two profiles are of different devices: /device:TPU:1 before, /device:TPU:2 now
where the time goes in v1:
time: 93.7 us; the launch traced here: 93.6 us
  Pallas kernels  92 us (98%)
  local copies, waits for them, and re-layouts  1.56 us (2%)
    pallas_call x1, Pallas kernels, local(): pl.pallas_call(kernel, out_shape=jax.ShapeDtypeStruct(vectors.shape, floa...  92 us

profile of v1, /device:TPU:2, one launch (start us, length us, event | category | flops | bytes accessed | tf_op | source)
XLA Modules:
  0.0 93.6 jit_solution(7219965382554667905)
XLA Ops:
  0.0 0.0 copy-start
  0.0 0.9 copy-done
  0.9 92.0 %shard_map.28 = f32[32,1024]{1,0:T(8,128)S(1)} custom-call(f32[1024,2048]{1,0:T(8,128)} %matrix_hbm.1, f32[32,1024]{1,0:T(8,128)S(1)} %copy-done), custom_call_target="tpu_custom_call" | custom-call | tf_op jit(solution)/shard_map/pallas_call | solution.py:276
  92.9 0.7 copy.4
Async XLA Ops:
  0.0 0.9 copy-start
